TPU v7x, 32 devices: a whole 2x2x4 slice. The times are simulated.
32 devices in a mesh: row: 8 (over z, y), col: 4 (over x, core).
Axes of the slice: x: 2, y: 2, z: 4, core: 2. Of those that a mesh axis runs over, the one named last changes fastest.
Arguments:
- right_side: float32 [3, 64, 512], P(None, 'row', 'col'), may hold values from -6 to 6
- viscosity: float32 [64, 512], P('row', 'col'), may hold values from 0.1 to 3
- free_mask: int32 [3, 64, 512], P(None, 'row', 'col'), may hold values 0 or 1
- coarse_basis: float32 [64, 3, 64, 512], P(None, None, 'row', 'col'), may hold values from -6 to 6
- gram_inverse: float32 [64, 64], P('col'), may hold values from -3 to 6, as said below
Outputs:
- solution: float32 [3, 64, 512], P(None, 'row', 'col')
- residual: float32 [3, 64, 512], P(None, 'row', 'col')
Inputs may be any that keep to these rules, and one draw needn't show every extreme that they name: `free_mask`: 1 marks a free velocity unknown, 0 one whose value is prescribed. `gram_inverse`: symmetric positive definite.
All inputs are finite; a program needn't handle non-finite values. No bound on the sum of `free_mask` on one device may be relied on, other than what follows from the above.
Results may differ from a plain program's by a relative error of at most 0.0003.
Values sent between devices are 32-bit elements; how exact they have to be, the bound alone decides.
A program may use at most 64 MiB of HBM per device.

v0:
```python
import math
import jax
import jax.numpy as jnp
from jax import lax
from jax.sharding import PartitionSpec as P

ITERS = 2


def padded_2(shard, sides, width):
    for axis, dim in sides:
        count, length = (lax.axis_size(axis), shard.shape[dim])
        up = [(i, (i + 1) % count) for i in range(count - 1)]
        down = [(j, i) for i, j in up]
        last = lax.slice_in_dim(shard, length - width, length, axis=dim)
        leading = lax.slice_in_dim(shard, 0, width, axis=dim)
        before = lax.ppermute(last, axis, up)
        after = lax.ppermute(leading, axis, down)
        shard = jnp.concatenate([before, shard, after], axis=dim)
    return shard


def on_device(right_side, viscosity, free_mask, coarse_basis, gram_inverse):
    high = lax.Precision.HIGHEST
    components, patch_rows, patch_cols = right_side.shape
    columns = coarse_basis.shape[0]
    unknowns = (
        components * patch_rows * patch_cols * lax.axis_size("row") * lax.axis_size("col") * columns
    )
    coarse_scale = 1.0 / (32.0 * math.sqrt(float(unknowns)))
    viscosity_pad = padded_2(viscosity, (("row", 0), ("col", 1)), 1)
    face_north = 0.5 * (viscosity + viscosity_pad[2:, 1:-1])
    face_south = 0.5 * (viscosity + viscosity_pad[:-2, 1:-1])
    face_east = 0.5 * (viscosity + viscosity_pad[1:-1, 2:])
    face_west = 0.5 * (viscosity + viscosity_pad[1:-1, :-2])
    diagonal = 1.0 + face_north + face_south + face_east + face_west
    unfixed = free_mask.astype(jnp.float32)
    jacobi = unfixed / diagonal + (1.0 - unfixed)
    basis_rows = coarse_basis.reshape(columns, -1)

    def solve_coarse(coarse_dot):
        coeff_part = jnp.dot(gram_inverse, coarse_dot, precision=high) * coarse_scale
        return lax.all_gather(coeff_part, "col", axis=0, tiled=True)

    def precondition(residual, coarse_dot, weighted_sq):
        coeffs = solve_coarse(coarse_dot)
        smoothed = jacobi * residual + jnp.dot(coeffs, basis_rows, precision=high).reshape(
            residual.shape
        )
        return (smoothed, weighted_sq + jnp.dot(coarse_dot, coeffs, precision=high))

    solution = jnp.zeros_like(right_side)
    residual = right_side
    coarse_dot, weighted_sq = lax.psum(
        (
            jnp.dot(basis_rows, residual.reshape(-1), precision=high),
            jnp.sum(jacobi * residual * residual),
        ),
        ("row", "col"),
    )
    direction, energy = precondition(residual, coarse_dot, weighted_sq)
    for iteration in range(ITERS):
        masked = unfixed * direction
        padded = padded_2(masked, (("row", 1), ("col", 2)), 1)
        stencil = diagonal * masked - (
            face_north * padded[:, 2:, 1:-1]
            + face_south * padded[:, :-2, 1:-1]
            + face_east * padded[:, 1:-1, 2:]
            + face_west * padded[:, 1:-1, :-2]
        )
        applied = unfixed * stencil + (1.0 - unfixed) * direction
        if iteration + 1 < ITERS:
            curve_sum, image_coarse, cross_term, image_sq = lax.psum(
                (
                    jnp.sum(direction * applied),
                    jnp.dot(basis_rows, applied.reshape(-1), precision=high),
                    jnp.sum(jacobi * residual * applied),
                    jnp.sum(jacobi * applied * applied),
                ),
                ("row", "col"),
            )
            step_len = energy / curve_sum
            solution = step_len * direction
            residual = residual - step_len * applied
            coarse_dot = coarse_dot - step_len * image_coarse
            weighted_sq = weighted_sq - 2.0 * step_len * cross_term + step_len * step_len * image_sq
            smoothed, energy_new = precondition(residual, coarse_dot, weighted_sq)
            direction = smoothed + energy_new / energy * direction
            energy = energy_new
        else:
            curve_sum = lax.psum(jnp.sum(direction * applied), ("row", "col"))
            step_len = energy / curve_sum
            solution = solution + step_len * direction
            residual = residual - step_len * applied
    return (solution, residual)


def solution(mesh):
    in_specs = (
        P(None, "row", "col"),
        P("row", "col"),
        P(None, "row", "col"),
        P(None, None, "row", "col"),
        P("col", None),
    )
    out_specs = (P(None, "row", "col"), P(None, "row", "col"))
    return jax.shard_map(
        on_device, mesh=mesh, in_specs=in_specs, out_specs=out_specs, check_vma=False
    )
```

profile of v0, /device:TPU:0, one launch (start us, length us, event | category | flops | bytes accessed | tf_op | source)
XLA Modules:
  0.0 198.3 jit_solution(4688476039508117926)
XLA Ops:
  1.4 1.3 collective-permute-start
  2.7 5.5 %collective-permute-start.1 = (f32[1,128]{1,0:T(1,128)S(1)}, f32[1,128]{1,0:T(1,128)S(1)}, u32[]{:S(2)}, u32[]{:S(2)}) collective-permute-start(f32[1,128]{1,0:T(1,128)S(1)} %get-tuple-element.33), channel_id=1, source_target_pairs={{0,4},{4,8},{8,12},{12,16},{16,20},{20,24},{24,28},{1,5},{5,9},{9,... | collective-permute-start | bytes 1544 | tf_op jit(solution)/shard_map/ppermute | solution.py:17
  8.2 1.3 copy.32
  9.7 1.0 copy-done.1
  11.4 41.9 %psum.50 = f32[64]{0:T(128)S(1)} all-reduce(f32[64]{0:T(128)S(1)} %convolution_bitcast_fusion.3), channel_id=1, replica_groups=mesh['row'=8,'col'=4] {'row','col'}, use_global_device_ids=true, to_apply=%region_2.0 | all-reduce | flops 64 | bytes 512 | tf_op jit(solution)/shard_map/psum | solution.py:54
  55.5 5.8 %all-reduce = f32[64]{0:T(128)S(1)} all-reduce(f32[64]{0:T(128)S(1)} %dynamic-update-slice), channel_id=1, replica_groups=mesh['row'=8,'col'=4] {'col'}, use_global_device_ids=true, to_apply=%add | all-reduce | flops 64 | bytes 512
  62.1 1.3 collective-permute-start.2
  63.4 3.0 %collective-permute-start.3 = (f32[10,1]{1,0:T(8,128)S(1)}, f32[10,1]{1,0:T(8,128)S(1)}, u32[]{:S(2)}, u32[]{:S(2)}) collective-permute-start(f32[10,1]{1,0:T(8,128)S(1)} %get-tuple-element.31), channel_id=1, source_target_pairs={{0,1},{1,2},{2,3},{4,5},{5,6},{6,7},{8,9},{9,10},{10,11},{12,13},{... | collective-permute-start | bytes 128 | tf_op jit(solution)/shard_map/ppermute | solution.py:17
  66.5 0.8 collective-permute-done.3
  67.4 1.3 collective-permute-start.4
  68.7 4.8 %collective-permute-start.5 = (f32[3,1,128]{2,1,0:T(1,128)S(1)}, f32[3,1,128]{2,1,0:T(1,128)S(1)}, u32[]{:S(2)}, u32[]{:S(2)}) collective-permute-start(f32[3,1,128]{2,1,0:T(1,128)S(1)} %get-tuple-element.29), channel_id=1, source_target_pairs={{0,4},{4,8},{8,12},{12,16},{16,20},{20,24},{24,28},{1,5},{5,9},{9,... | collective-permute-start | bytes 4616 | tf_op jit(solution)/shard_map/ppermute | solution.py:17
  73.5 1.3 collective-permute-done.5
  74.9 2.3 %collective-permute-start.7 = (f32[3,10,1]{2,1,0:T(8,128)S(1)}, f32[3,10,1]{2,1,0:T(8,128)S(1)}, u32[]{:S(2)}, u32[]{:S(2)}) collective-permute-start(f32[3,10,1]{2,1,0:T(8,128)S(1)} %get-tuple-element.26), channel_id=1, source_target_pairs={{0,1},{1,2},{2,3},{4,5},{5,6},{6,7},{8,9},{9,10},{10,11},{12,13},{... | collective-permute-start | bytes 368 | tf_op jit(solution)/shard_map/ppermute | solution.py:17
  77.2 1.3 collective-permute-start.6
  79.1 4.0 %collective-permute-done.6 = f32[3,10,1]{2,1,0:T(8,128)S(1)} collective-permute-done((f32[3,10,1]{2,1,0:T(8,128)S(1)}, f32[3,10,1]{2,1,0:T(8,128)S(1)}, u32[]{:S(2)}, u32[]{:S(2)}) %collective-permute-start.6) | collective-permute-done | bytes 152 | tf_op jit(solution)/shard_map/ppermute | solution.py:18
  84.6 42.6 %all-reduce.2 = (f32[64]{0:T(128)S(1)}, f32[]{:T(128)}, f32[]{:T(128)}, f32[]{:T(128)}, f32[]{:T(128)}) all-reduce(f32[64]{0:T(128)S(1)} %convolution_bitcast_fusion.1, f32[]{:T(128)} %get-tuple-element.4, f32[]{:T(128)} %get-tuple-element.5, f32[]{:T(128)} %get-tuple-element.3, ...), channel_id=1, replica_groups=mesh['row'=8,'col'=4] {'row','col'}, use_global_device_ids=true, to_apply=%region_9.0 | all-reduce | flops 68 | bytes 544 | tf_op jit(solution)/shard_map/psum | solution.py:73
  129.5 7.6 %all-reduce.1 = f32[64]{0:T(128)S(1)} all-reduce(f32[64]{0:T(128)S(1)} %dynamic-update-slice.1), channel_id=1, replica_groups=mesh['row'=8,'col'=4] {'col'}, use_global_device_ids=true, to_apply=%add.1 | all-reduce | flops 64 | bytes 512
  140.8 1.3 collective-permute-start.8
  142.1 4.5 %collective-permute-start.9 = (f32[3,1,128]{2,1,0:T(1,128)S(1)}, f32[3,1,128]{2,1,0:T(1,128)S(1)}, u32[]{:S(2)}, u32[]{:S(2)}) collective-permute-start(f32[3,1,128]{2,1,0:T(1,128)S(1)} %get-tuple-element.27), channel_id=1, source_target_pairs={{0,4},{4,8},{8,12},{12,16},{16,20},{20,24},{24,28},{1,5},{5,9},{9,... | collective-permute-start | bytes 4616 | tf_op jit(solution)/shard_map/ppermute | solution.py:17
  146.7 1.3 collective-permute-done.9
  148.0 1.3 collective-permute-start.11
  149.3 1.3 collective-permute-start.10
  150.6 2.6 %collective-permute-done.10 = f32[3,10,1]{2,1,0:T(8,128)S(1)} collective-permute-done((f32[3,10,1]{2,1,0:T(8,128)S(1)}, f32[3,10,1]{2,1,0:T(8,128)S(1)}, u32[]{:S(2)}, u32[]{:S(2)}) %collective-permute-start.10) | collective-permute-done | bytes 152 | tf_op jit(solution)/shard_map/ppermute | solution.py:18
  154.0 43.0 %psum.55 = f32[]{:T(128)} all-reduce(f32[]{:T(128)} %get-tuple-element.11), channel_id=1, replica_groups=mesh['row'=8,'col'=4] {'row','col'}, use_global_device_ids=true, to_apply=%region_11.0 | all-reduce | flops 1 | bytes 8 | tf_op jit(solution)/shard_map/psum | solution.py:91
  (47 shorter events, 9.3 us)
Async XLA Ops:
  0.6 52.6 %copy-start = (f32[16,64]{1,0:T(8,128)S(1)}, f32[16,64]{1,0:T(8,128)}, u32[]{:S(2)}) copy-start(f32[16,64]{1,0:T(8,128)} %param.9) | copy-start | bytes 12292
  1.4 60.5 %collective-permute-start = (f32[1,128]{1,0:T(1,128)S(1)}, f32[1,128]{1,0:T(1,128)S(1)}, u32[]{:S(2)}, u32[]{:S(2)}) collective-permute-start(f32[1,128]{1,0:T(1,128)S(1)} %get-tuple-element.34), channel_id=1, source_target_pairs={{4,0},{8,4},{12,8},{16,12},{20,16},{24,20},{28,24},{5,1},{9,5},{13... | collective-permute-start | bytes 1544 | tf_op jit(solution)/shard_map/ppermute | solution.py:18
  2.7 59.2 %collective-permute-start.1 = (f32[1,128]{1,0:T(1,128)S(1)}, f32[1,128]{1,0:T(1,128)S(1)}, u32[]{:S(2)}, u32[]{:S(2)}) collective-permute-start(f32[1,128]{1,0:T(1,128)S(1)} %get-tuple-element.33), channel_id=1, source_target_pairs={{0,4},{4,8},{8,12},{12,16},{16,20},{20,24},{24,28},{1,5},{5,9},{9,... | collective-permute-start | bytes 1544 | tf_op jit(solution)/shard_map/ppermute | solution.py:17
  9.5 1.1 copy-start.1
  9.5 1.1 copy-start.2
  53.4 0.7 copy-start.5
  61.3 0.7 copy-start.4
  62.0 5.3 %copy-start.3 = (s32[3,8,128]{2,1,0:T(8,128)S(1)}, s32[3,8,128]{2,1,0:T(8,128)}, u32[]{:S(2)}) copy-start(s32[3,8,128]{2,1,0:T(8,128)} %param.7) | copy-start | bytes 36868
  62.1 4.3 %collective-permute-start.2 = (f32[10,1]{1,0:T(8,128)S(1)}, f32[10,1]{1,0:T(8,128)S(1)}, u32[]{:S(2)}, u32[]{:S(2)}) collective-permute-start(f32[10,1]{1,0:T(8,128)S(1)} %get-tuple-element.32), channel_id=1, source_target_pairs={{1,0},{2,1},{3,2},{5,4},{6,5},{7,6},{9,8},{10,9},{11,10},{13,12},{... | collective-permute-start | bytes 128 | tf_op jit(solution)/shard_map/ppermute | solution.py:18
  63.4 3.8 %collective-permute-start.3 = (f32[10,1]{1,0:T(8,128)S(1)}, f32[10,1]{1,0:T(8,128)S(1)}, u32[]{:S(2)}, u32[]{:S(2)}) collective-permute-start(f32[10,1]{1,0:T(8,128)S(1)} %get-tuple-element.31), channel_id=1, source_target_pairs={{0,1},{1,2},{2,3},{4,5},{5,6},{6,7},{8,9},{9,10},{10,11},{12,13},{... | collective-permute-start | bytes 128 | tf_op jit(solution)/shard_map/ppermute | solution.py:17
  67.4 6.1 %collective-permute-start.4 = (f32[3,1,128]{2,1,0:T(1,128)S(1)}, f32[3,1,128]{2,1,0:T(1,128)S(1)}, u32[]{:S(2)}, u32[]{:S(2)}) collective-permute-start(f32[3,1,128]{2,1,0:T(1,128)S(1)} %get-tuple-element.30), channel_id=1, source_target_pairs={{4,0},{8,4},{12,8},{16,12},{20,16},{24,20},{28,24},{5,1},{9,5},{13... | collective-permute-start | bytes 4616 | tf_op jit(solution)/shard_map/ppermute | solution.py:18
  68.7 6.1 %collective-permute-start.5 = (f32[3,1,128]{2,1,0:T(1,128)S(1)}, f32[3,1,128]{2,1,0:T(1,128)S(1)}, u32[]{:S(2)}, u32[]{:S(2)}) collective-permute-start(f32[3,1,128]{2,1,0:T(1,128)S(1)} %get-tuple-element.29), channel_id=1, source_target_pairs={{0,4},{4,8},{8,12},{12,16},{16,20},{20,24},{24,28},{1,5},{5,9},{9,... | collective-permute-start | bytes 4616 | tf_op jit(solution)/shard_map/ppermute | solution.py:17
  74.9 4.3 %collective-permute-start.7 = (f32[3,10,1]{2,1,0:T(8,128)S(1)}, f32[3,10,1]{2,1,0:T(8,128)S(1)}, u32[]{:S(2)}, u32[]{:S(2)}) collective-permute-start(f32[3,10,1]{2,1,0:T(8,128)S(1)} %get-tuple-element.26), channel_id=1, source_target_pairs={{0,1},{1,2},{2,3},{4,5},{5,6},{6,7},{8,9},{9,10},{10,11},{12,13},{... | collective-permute-start | bytes 368 | tf_op jit(solution)/shard_map/ppermute | solution.py:17
  77.2 6.0 %collective-permute-start.6 = (f32[3,10,1]{2,1,0:T(8,128)S(1)}, f32[3,10,1]{2,1,0:T(8,128)S(1)}, u32[]{:S(2)}, u32[]{:S(2)}) collective-permute-start(f32[3,10,1]{2,1,0:T(8,128)S(1)} %get-tuple-element.25), channel_id=1, source_target_pairs={{1,0},{2,1},{3,2},{5,4},{6,5},{7,6},{9,8},{10,9},{11,10},{13,12},{... | collective-permute-start | bytes 368 | tf_op jit(solution)/shard_map/ppermute | solution.py:18
  140.8 5.9 %collective-permute-start.8 = (f32[3,1,128]{2,1,0:T(1,128)S(1)}, f32[3,1,128]{2,1,0:T(1,128)S(1)}, u32[]{:S(2)}, u32[]{:S(2)}) collective-permute-start(f32[3,1,128]{2,1,0:T(1,128)S(1)} %get-tuple-element.28), channel_id=1, source_target_pairs={{4,0},{8,4},{12,8},{16,12},{20,16},{24,20},{28,24},{5,1},{9,5},{13... | collective-permute-start | bytes 4616 | tf_op jit(solution)/shard_map/ppermute | solution.py:18
  142.1 5.8 %collective-permute-start.9 = (f32[3,1,128]{2,1,0:T(1,128)S(1)}, f32[3,1,128]{2,1,0:T(1,128)S(1)}, u32[]{:S(2)}, u32[]{:S(2)}) collective-permute-start(f32[3,1,128]{2,1,0:T(1,128)S(1)} %get-tuple-element.27), channel_id=1, source_target_pairs={{0,4},{4,8},{8,12},{12,16},{16,20},{20,24},{24,28},{1,5},{5,9},{9,... | collective-permute-start | bytes 4616 | tf_op jit(solution)/shard_map/ppermute | solution.py:17
  148.0 2.6 %collective-permute-start.11 = (f32[3,10,1]{2,1,0:T(8,128)S(1)}, f32[3,10,1]{2,1,0:T(8,128)S(1)}, u32[]{:S(2)}, u32[]{:S(2)}) collective-permute-start(f32[3,10,1]{2,1,0:T(8,128)S(1)} %get-tuple-element.24), channel_id=1, source_target_pairs={{0,1},{1,2},{2,3},{4,5},{5,6},{6,7},{8,9},{9,10},{10,11},{12,13},{... | collective-permute-start | bytes 368 | tf_op jit(solution)/shard_map/ppermute | solution.py:17
  149.3 3.9 %collective-permute-start.10 = (f32[3,10,1]{2,1,0:T(8,128)S(1)}, f32[3,10,1]{2,1,0:T(8,128)S(1)}, u32[]{:S(2)}, u32[]{:S(2)}) collective-permute-start(f32[3,10,1]{2,1,0:T(8,128)S(1)} %get-tuple-element.23), channel_id=1, source_target_pairs={{1,0},{2,1},{3,2},{5,4},{6,5},{7,6},{9,8},{10,9},{11,10},{13,12},{... | collective-permute-start | bytes 368 | tf_op jit(solution)/shard_map/ppermute | solution.py:18
where the time goes:
time: 199 us; the launch traced here: 198 us
  blocking collectives  141 us (71%)
  starting transfers between devices  29.2 us (15%)
  waiting for transfers between devices  10 us (5%)
  between operations  6.67 us (3%)
  local copies, waits for them, and re-layouts  5.22 us (3%)
  other arithmetic  3.45 us (2%)
  matrix products  2.83 us (1%)
    psum x1, blocking collectives, on_device(): curve_sum = lax.psum(jnp.sum(direction * applied), ('row', 'col'))  43 us
    psum x1, blocking collectives, on_device(): lax.psum((jnp.sum(direction * applied), jnp.dot(basis_rows, applied.resha...  42.6 us
    psum x1, blocking collectives, on_device(): lax.psum((jnp.dot(basis_rows, residual.reshape(-1), precision=high), jnp....  41.9 us
    ppermute x6, starting transfers between devices, padded_2(): before = lax.ppermute(last, axis, up)  21.5 us
    unnamed x2, blocking collectives  13.4 us
    ppermute x6, starting transfers between devices, padded_2(): after = lax.ppermute(leading, axis, down)  7.73 us
    ppermute x6, waiting for transfers between devices, padded_2(): after = lax.ppermute(leading, axis, down)  6.67 us
    unnamed x19, local copies, waits for them, and re-layouts  4.22 us
  transfers between devices with their start and end apart: 12, of which 5 were waited for; matrix products, arithmetic and copies ran while one was open for 2% of the time, Pallas kernels for 0%

commit v1 on v0

--- a/solution.py
+++ b/solution.py
@@ -51,12 +51,14 @@
 
     solution = jnp.zeros_like(right_side)
     residual = right_side
-    coarse_dot, weighted_sq = lax.psum(
+    _play_yards = lambda xx, a_name, axis_tag: lax.psum(lax.psum(xx, a_name), axis_tag)
+    coarse_dot, weighted_sq = _play_yards(
         (
             jnp.dot(basis_rows, residual.reshape(-1), precision=high),
             jnp.sum(jacobi * residual * residual),
         ),
-        ("row", "col"),
+        "col",
+        "row",
     )
     direction, energy = precondition(residual, coarse_dot, weighted_sq)
     for iteration in range(ITERS):

time: 199 us -> 208 us (1.045)
  blocking collectives: 141 us -> 149 us
    psum x1 -> x4, blocking collectives: 41.9 us -> 55.2 us  [the longest x2 39.8 us: on_device(): lax.psum(lax.psum(xx, a_name), axis_tag)]
    psum x1, blocking collectives: 42.6 us -> 37.3 us  [on_device(): lax.psum((jnp.sum(direction * applied), jnp.dot(basis_rows, applied.resha...]
where the time goes in v1:
time: 208 us; the launch traced here: 207 us
  blocking collectives  149 us (72%)
  starting transfers between devices  28.5 us (14%)
  waiting for transfers between devices  11.2 us (5%)
  between operations  6.74 us (3%)
  local copies, waits for them, and re-layouts  5.22 us (3%)
  other arithmetic  3.45 us (2%)
  matrix products  2.83 us (1%)
    psum x1, blocking collectives, on_device(): curve_sum = lax.psum(jnp.sum(direction * applied), ('row', 'col'))  44.3 us
    psum x2, blocking collectives, on_device(): lax.psum(lax.psum(xx, a_name), axis_tag)  39.8 us
    psum x1, blocking collectives, on_device(): lax.psum((jnp.sum(direction * applied), jnp.dot(basis_rows, applied.resha...  37.3 us
    ppermute x6, starting transfers between devices, padded_2(): before = lax.ppermute(last, axis, up)  20.8 us
    psum x2, blocking collectives, on_device(): lax.psum(xx, a_name)  15.3 us
    unnamed x2, blocking collectives  12.5 us
    ppermute x6, waiting for transfers between devices, padded_2(): after = lax.ppermute(leading, axis, down)  7.88 us
    ppermute x6, starting transfers between devices, padded_2(): after = lax.ppermute(leading, axis, down)  7.73 us
  transfers between devices with their start and end apart: 12, of which 5 were waited for; matrix products, arithmetic and copies ran while one was open for 2% of the time, Pallas kernels for 0%

profile of v1, /device:TPU:0, one launch (start us, length us, event | category | flops | bytes accessed | tf_op | source)
XLA Modules:
  0.0 207.2 jit_solution(10395584745322814752)
XLA Ops:
  1.4 1.3 collective-permute-start
  2.7 5.5 %collective-permute-start.1 = (f32[1,128]{1,0:T(1,128)S(1)}, f32[1,128]{1,0:T(1,128)S(1)}, u32[]{:S(2)}, u32[]{:S(2)}) collective-permute-start(f32[1,128]{1,0:T(1,128)S(1)} %get-tuple-element.32), channel_id=1, source_target_pairs={{0,4},{4,8},{8,12},{12,16},{16,20},{20,24},{24,28},{1,5},{5,9},{9,... | collective-permute-start | bytes 1544 | tf_op jit(solution)/shard_map/ppermute | solution.py:17
  8.2 1.3 copy.32
  11.4 6.5 %psum.65 = f32[64]{0:T(128)S(1)} all-reduce(f32[64]{0:T(128)S(1)} %convolution_bitcast_fusion.3), channel_id=1, replica_groups=mesh['row'=8,'col'=4] {'col'}, use_global_device_ids=true, to_apply=%region_3.0 | all-reduce | flops 64 | bytes 512 | tf_op jit(solution)/shard_map/psum | solution.py:54
  17.9 19.8 %psum.66 = f32[64]{0:T(128)S(1)} all-reduce(f32[64]{0:T(128)S(1)} %psum.65), channel_id=1, replica_groups=mesh['row'=8,'col'=4] {'row'}, use_global_device_ids=true, to_apply=%region_4.0 | all-reduce | flops 64 | bytes 512 | tf_op jit(solution)/shard_map/psum | solution.py:54
  40.0 5.6 %all-reduce = f32[64]{0:T(128)S(1)} all-reduce(f32[64]{0:T(128)S(1)} %dynamic-update-slice), channel_id=1, replica_groups=mesh['row'=8,'col'=4] {'col'}, use_global_device_ids=true, to_apply=%add | all-reduce | flops 64 | bytes 512
  46.4 1.3 collective-permute-start.2
  47.7 3.0 %collective-permute-start.3 = (f32[10,1]{1,0:T(8,128)S(1)}, f32[10,1]{1,0:T(8,128)S(1)}, u32[]{:S(2)}, u32[]{:S(2)}) collective-permute-start(f32[10,1]{1,0:T(8,128)S(1)} %get-tuple-element.30), channel_id=1, source_target_pairs={{0,1},{1,2},{2,3},{4,5},{5,6},{6,7},{8,9},{9,10},{10,11},{12,13},{... | collective-permute-start | bytes 128 | tf_op jit(solution)/shard_map/ppermute | solution.py:17
  51.6 1.3 collective-permute-start.4
  52.9 4.5 %collective-permute-start.5 = (f32[3,1,128]{2,1,0:T(1,128)S(1)}, f32[3,1,128]{2,1,0:T(1,128)S(1)}, u32[]{:S(2)}, u32[]{:S(2)}) collective-permute-start(f32[3,1,128]{2,1,0:T(1,128)S(1)} %get-tuple-element.28), channel_id=1, source_target_pairs={{0,4},{4,8},{8,12},{12,16},{16,20},{20,24},{24,28},{1,5},{5,9},{9,... | collective-permute-start | bytes 4616 | tf_op jit(solution)/shard_map/ppermute | solution.py:17
  58.9 1.8 collective-permute-start.7
  60.7 1.3 collective-permute-start.6
  62.0 4.7 %collective-permute-done.6 = f32[3,10,1]{2,1,0:T(8,128)S(1)} collective-permute-done((f32[3,10,1]{2,1,0:T(8,128)S(1)}, f32[3,10,1]{2,1,0:T(8,128)S(1)}, u32[]{:S(2)}, u32[]{:S(2)}) %collective-permute-start.6) | collective-permute-done | bytes 152 | tf_op jit(solution)/shard_map/ppermute | solution.py:18
  67.5 8.8 %psum.63 = f32[]{:T(128)} all-reduce(f32[]{:T(128)} %get-tuple-element.4), channel_id=1, replica_groups=mesh['row'=8,'col'=4] {'col'}, use_global_device_ids=true, to_apply=%region_1.0 | all-reduce | flops 1 | bytes 8 | tf_op jit(solution)/shard_map/psum | solution.py:54
  77.0 20.0 %psum.64 = f32[]{:T(128)} all-reduce(f32[]{:T(128)} %psum.63), channel_id=1, replica_groups=mesh['row'=8,'col'=4] {'row'}, use_global_device_ids=true, to_apply=%region_2.0 | all-reduce | flops 1 | bytes 8 | tf_op jit(solution)/shard_map/psum | solution.py:54
  99.0 37.3 %all-reduce.2 = (f32[64]{0:T(128)S(1)}, f32[]{:T(128)}, f32[]{:T(128)}, f32[]{:T(128)}) all-reduce(f32[64]{0:T(128)S(1)} %convolution_bitcast_fusion.1, f32[]{:T(128)} %get-tuple-element.5, f32[]{:T(128)} %get-tuple-element.3, f32[]{:T(128)} %get-tuple-element.2), channel_id=1, replica_groups=mesh['row'=8,'col'=4] {'row','col'}, use_global_device_ids=true, to_apply=%region_11.0 | all-reduce | flops 67 | bytes 536 | tf_op jit(solution)/shard_map/psum | solution.py:75
  137.3 6.9 %all-reduce.1 = f32[64]{0:T(128)S(1)} all-reduce(f32[64]{0:T(128)S(1)} %dynamic-update-slice.1), channel_id=1, replica_groups=mesh['row'=8,'col'=4] {'col'}, use_global_device_ids=true, to_apply=%add.1 | all-reduce | flops 64 | bytes 512
  147.9 1.3 collective-permute-start.8
  149.2 4.5 %collective-permute-start.9 = (f32[3,1,128]{2,1,0:T(1,128)S(1)}, f32[3,1,128]{2,1,0:T(1,128)S(1)}, u32[]{:S(2)}, u32[]{:S(2)}) collective-permute-start(f32[3,1,128]{2,1,0:T(1,128)S(1)} %get-tuple-element.26), channel_id=1, source_target_pairs={{0,4},{4,8},{8,12},{12,16},{16,20},{20,24},{24,28},{1,5},{5,9},{9,... | collective-permute-start | bytes 4616 | tf_op jit(solution)/shard_map/ppermute | solution.py:17
  153.8 1.3 collective-permute-done.9
  155.2 1.3 collective-permute-start.11
  156.5 1.3 collective-permute-start.10
  157.8 3.2 %collective-permute-done.10 = f32[3,10,1]{2,1,0:T(8,128)S(1)} collective-permute-done((f32[3,10,1]{2,1,0:T(8,128)S(1)}, f32[3,10,1]{2,1,0:T(8,128)S(1)}, u32[]{:S(2)}, u32[]{:S(2)}) %collective-permute-start.10) | collective-permute-done | bytes 152 | tf_op jit(solution)/shard_map/ppermute | solution.py:18
  161.6 44.3 %psum.71 = f32[]{:T(128)} all-reduce(f32[]{:T(128)} %get-tuple-element.10), channel_id=1, replica_groups=mesh['row'=8,'col'=4] {'row','col'}, use_global_device_ids=true, to_apply=%region_13.0 | all-reduce | flops 1 | bytes 8 | tf_op jit(solution)/shard_map/psum | solution.py:93
  (50 shorter events, 12.3 us)
Async XLA Ops:
  0.6 37.1 %copy-start = (f32[16,64]{1,0:T(8,128)S(1)}, f32[16,64]{1,0:T(8,128)}, u32[]{:S(2)}) copy-start(f32[16,64]{1,0:T(8,128)} %param.9) | copy-start | bytes 12292
  1.4 44.8 %collective-permute-start = (f32[1,128]{1,0:T(1,128)S(1)}, f32[1,128]{1,0:T(1,128)S(1)}, u32[]{:S(2)}, u32[]{:S(2)}) collective-permute-start(f32[1,128]{1,0:T(1,128)S(1)} %get-tuple-element.33), channel_id=1, source_target_pairs={{4,0},{8,4},{12,8},{16,12},{20,16},{24,20},{28,24},{5,1},{9,5},{13... | collective-permute-start | bytes 1544 | tf_op jit(solution)/shard_map/ppermute | solution.py:18
  2.7 43.5 %collective-permute-start.1 = (f32[1,128]{1,0:T(1,128)S(1)}, f32[1,128]{1,0:T(1,128)S(1)}, u32[]{:S(2)}, u32[]{:S(2)}) collective-permute-start(f32[1,128]{1,0:T(1,128)S(1)} %get-tuple-element.32), channel_id=1, source_target_pairs={{0,4},{4,8},{8,12},{12,16},{16,20},{20,24},{24,28},{1,5},{5,9},{9,... | collective-permute-start | bytes 1544 | tf_op jit(solution)/shard_map/ppermute | solution.py:17
  9.5 1.1 copy-start.1
  9.5 1.1 copy-start.2
  37.8 0.7 copy-start.5
  45.6 0.7 copy-start.4
  46.3 5.3 %copy-start.3 = (s32[3,8,128]{2,1,0:T(8,128)S(1)}, s32[3,8,128]{2,1,0:T(8,128)}, u32[]{:S(2)}) copy-start(s32[3,8,128]{2,1,0:T(8,128)} %param.7) | copy-start | bytes 36868
  46.4 4.3 %collective-permute-start.2 = (f32[10,1]{1,0:T(8,128)S(1)}, f32[10,1]{1,0:T(8,128)S(1)}, u32[]{:S(2)}, u32[]{:S(2)}) collective-permute-start(f32[10,1]{1,0:T(8,128)S(1)} %get-tuple-element.31), channel_id=1, source_target_pairs={{1,0},{2,1},{3,2},{5,4},{6,5},{7,6},{9,8},{10,9},{11,10},{13,12},{... | collective-permute-start | bytes 128 | tf_op jit(solution)/shard_map/ppermute | solution.py:18
  47.7 3.8 %collective-permute-start.3 = (f32[10,1]{1,0:T(8,128)S(1)}, f32[10,1]{1,0:T(8,128)S(1)}, u32[]{:S(2)}, u32[]{:S(2)}) collective-permute-start(f32[10,1]{1,0:T(8,128)S(1)} %get-tuple-element.30), channel_id=1, source_target_pairs={{0,1},{1,2},{2,3},{4,5},{5,6},{6,7},{8,9},{9,10},{10,11},{12,13},{... | collective-permute-start | bytes 128 | tf_op jit(solution)/shard_map/ppermute | solution.py:17
  51.6 5.9 %collective-permute-start.4 = (f32[3,1,128]{2,1,0:T(1,128)S(1)}, f32[3,1,128]{2,1,0:T(1,128)S(1)}, u32[]{:S(2)}, u32[]{:S(2)}) collective-permute-start(f32[3,1,128]{2,1,0:T(1,128)S(1)} %get-tuple-element.29), channel_id=1, source_target_pairs={{4,0},{8,4},{12,8},{16,12},{20,16},{24,20},{28,24},{5,1},{9,5},{13... | collective-permute-start | bytes 4616 | tf_op jit(solution)/shard_map/ppermute | solution.py:18
  52.9 5.8 %collective-permute-start.5 = (f32[3,1,128]{2,1,0:T(1,128)S(1)}, f32[3,1,128]{2,1,0:T(1,128)S(1)}, u32[]{:S(2)}, u32[]{:S(2)}) collective-permute-start(f32[3,1,128]{2,1,0:T(1,128)S(1)} %get-tuple-element.28), channel_id=1, source_target_pairs={{0,4},{4,8},{8,12},{12,16},{16,20},{20,24},{24,28},{1,5},{5,9},{9,... | collective-permute-start | bytes 4616 | tf_op jit(solution)/shard_map/ppermute | solution.py:17
  58.9 3.1 %collective-permute-start.7 = (f32[3,10,1]{2,1,0:T(8,128)S(1)}, f32[3,10,1]{2,1,0:T(8,128)S(1)}, u32[]{:S(2)}, u32[]{:S(2)}) collective-permute-start(f32[3,10,1]{2,1,0:T(8,128)S(1)} %get-tuple-element.25), channel_id=1, source_target_pairs={{0,1},{1,2},{2,3},{4,5},{5,6},{6,7},{8,9},{9,10},{10,11},{12,13},{... | collective-permute-start | bytes 368 | tf_op jit(solution)/shard_map/ppermute | solution.py:17
  60.7 6.0 %collective-permute-start.6 = (f32[3,10,1]{2,1,0:T(8,128)S(1)}, f32[3,10,1]{2,1,0:T(8,128)S(1)}, u32[]{:S(2)}, u32[]{:S(2)}) collective-permute-start(f32[3,10,1]{2,1,0:T(8,128)S(1)} %get-tuple-element.24), channel_id=1, source_target_pairs={{1,0},{2,1},{3,2},{5,4},{6,5},{7,6},{9,8},{10,9},{11,10},{13,12},{... | collective-permute-start | bytes 368 | tf_op jit(solution)/shard_map/ppermute | solution.py:18
  147.9 5.9 %collective-permute-start.8 = (f32[3,1,128]{2,1,0:T(1,128)S(1)}, f32[3,1,128]{2,1,0:T(1,128)S(1)}, u32[]{:S(2)}, u32[]{:S(2)}) collective-permute-start(f32[3,1,128]{2,1,0:T(1,128)S(1)} %get-tuple-element.27), channel_id=1, source_target_pairs={{4,0},{8,4},{12,8},{16,12},{20,16},{24,20},{28,24},{5,1},{9,5},{13... | collective-permute-start | bytes 4616 | tf_op jit(solution)/shard_map/ppermute | solution.py:18
  149.2 5.8 %collective-permute-start.9 = (f32[3,1,128]{2,1,0:T(1,128)S(1)}, f32[3,1,128]{2,1,0:T(1,128)S(1)}, u32[]{:S(2)}, u32[]{:S(2)}) collective-permute-start(f32[3,1,128]{2,1,0:T(1,128)S(1)} %get-tuple-element.26), channel_id=1, source_target_pairs={{0,4},{4,8},{8,12},{12,16},{16,20},{20,24},{24,28},{1,5},{5,9},{9,... | collective-permute-start | bytes 4616 | tf_op jit(solution)/shard_map/ppermute | solution.py:17
  155.2 2.6 %collective-permute-start.11 = (f32[3,10,1]{2,1,0:T(8,128)S(1)}, f32[3,10,1]{2,1,0:T(8,128)S(1)}, u32[]{:S(2)}, u32[]{:S(2)}) collective-permute-start(f32[3,10,1]{2,1,0:T(8,128)S(1)} %get-tuple-element.23), channel_id=1, source_target_pairs={{0,1},{1,2},{2,3},{4,5},{5,6},{6,7},{8,9},{9,10},{10,11},{12,13},{... | collective-permute-start | bytes 368 | tf_op jit(solution)/shard_map/ppermute | solution.py:17
  156.5 4.5 %collective-permute-start.10 = (f32[3,10,1]{2,1,0:T(8,128)S(1)}, f32[3,10,1]{2,1,0:T(8,128)S(1)}, u32[]{:S(2)}, u32[]{:S(2)}) collective-permute-start(f32[3,10,1]{2,1,0:T(8,128)S(1)} %get-tuple-element.22), channel_id=1, source_target_pairs={{1,0},{2,1},{3,2},{5,4},{6,5},{7,6},{9,8},{10,9},{11,10},{13,12},{... | collective-permute-start | bytes 368 | tf_op jit(solution)/shard_map/ppermute | solution.py:18
